TPU v7x, 32 devices: a whole 2x2x4 slice. The times are simulated.
32 devices in a mesh: sec: 16 (over z, y, x), tile: 2 (over core).
Axes of the slice: x: 2, y: 2, z: 4, core: 2. Of those that a mesh axis runs over, the one named last changes fastest.
Arguments:
- image: bfloat16 [16, 512, 384], P('sec', 'tile'), may hold values from -12 to 12
- field: float32 [16, 2, 512, 384], P('sec', None, 'tile'), may hold values from -1.5 to 1.5
- displacement: int32 [4, 16, 2, 2], replicated, may hold values from -1 to 1
Outputs:
- aligned: float32 [16, 2, 512, 384], P('sec', None, 'tile')
All inputs are finite; a program needn't handle non-finite values.
Results may differ from a plain program's by a relative error of at most 0.01.
The roundings to bfloat16 on the way count: a program that leaves them out, or rounds other values in their place, can miss the bound.
Values may be sent and summed in bfloat16 or wider, within the bound.
A program may use at most 64 MiB of HBM per device.

v0:
```python
import jax
import jax.numpy as jnp
from jax import lax
from jax.sharding import PartitionSpec as P

BLOCK = 128
ITERS = 4


charb_eps2 = 0.25
step_size = 0.2
smooth_weight = 0.5


def with_halo(shard, sides, width):
    for axis, dim in sides:
        count, length = (lax.axis_size(axis), shard.shape[dim])
        up = [(i, (i + 1) % count) for i in range(count - 1)]
        down = [(j, i) for i, j in up]
        last = lax.slice_in_dim(shard, length - width, length, axis=dim)
        leading = lax.slice_in_dim(shard, 0, width, axis=dim)
        before = lax.ppermute(last, axis, up)
        after = lax.ppermute(leading, axis, down)
        shard = jnp.concatenate([before, shard, after], axis=dim)
    return shard


def passed_along(value, axis, steps):
    count = lax.axis_size(axis)
    leading, last = (max(0, -steps), min(count, count - steps))
    return lax.ppermute(value, axis, [(source, source + steps) for source in range(leading, last)])


def per_device(image, field, displacement):
    rows = image.shape[1]
    width = image.shape[2]
    sections = lax.axis_size("sec")
    height = rows * lax.axis_size("tile")
    section = lax.axis_index("sec")
    first_row = lax.axis_index("tile") * rows
    row_ids = first_row + jnp.arange(rows, dtype=jnp.int32)
    col_ids = jnp.arange(width, dtype=jnp.int32)
    section_ids = jnp.arange(sections, dtype=jnp.int32)
    rim_rows = with_halo(image[0], (("tile", 0),), 1).astype(jnp.float32)
    grad_rows = 0.5 * (rim_rows[2:] - rim_rows[:-2])
    plane = rim_rows[1:-1]
    side_pad = jnp.pad(plane, ((0, 0), (1, 1)))
    grad_cols = 0.5 * (side_pad[:, 2:] - side_pad[:, :-2])

    def inside_local(down, across):
        row_pos = row_ids + BLOCK * down
        col_pos = col_ids + BLOCK * across
        good_rows = ((row_pos >= 0) & (row_pos < height)).astype(jnp.float32)
        good_cols = ((col_pos >= 0) & (col_pos < width)).astype(jnp.float32)
        return good_rows[:, None] * good_cols[None, :]

    def move_local(extended, down, across):
        chosen = lax.dynamic_slice_in_dim(extended, BLOCK + BLOCK * down, rows, 0)
        widened = jnp.pad(chosen, ((0, 0), (BLOCK, BLOCK)))
        return lax.dynamic_slice_in_dim(widened, BLOCK + BLOCK * across, width, 1)

    current = field[0]
    for turn in range(ITERS):
        warped = (plane + grad_rows * current[0] + grad_cols * current[1]).astype(jnp.bfloat16)
        values = warped.astype(jnp.float32)
        table = displacement[turn]

        def fetch(offset):
            arrived = passed_along(warped, "sec", offset)
            return with_halo(arrived, (("tile", 0),), BLOCK)

        combined = jnp.zeros((rows, width), jnp.float32)
        energy = jnp.zeros((), jnp.float32)
        count = jnp.zeros((), jnp.int32)
        own_pairs = lax.dynamic_index_in_dim(table, section, 0, keepdims=False)
        for spacing in (1, 2):
            down = own_pairs[spacing - 1, 0]
            across = own_pairs[spacing - 1, 1]
            exists = (section + spacing < sections).astype(jnp.float32)
            moved = move_local(fetch(-spacing), down, across).astype(jnp.float32)
            mask = inside_local(down, across) * exists
            resid = mask * (values - moved)
            scaled = resid / jnp.sqrt(resid * resid + charb_eps2)
            energy = energy + jnp.sum(scaled * resid)
            all_rows = table[:, spacing - 1, 0]
            all_cols = table[:, spacing - 1, 1]
            count = count + jnp.sum(
                (section_ids + spacing < sections).astype(jnp.int32)
                * (height - BLOCK * jnp.abs(all_rows))
                * (width - BLOCK * jnp.abs(all_cols))
            )
            before_pairs = lax.dynamic_index_in_dim(
                table, jnp.maximum(section - spacing, 0), 0, keepdims=False
            )
            before_down = before_pairs[spacing - 1, 0]
            before_across = before_pairs[spacing - 1, 1]
            has_before = (section >= spacing).astype(jnp.float32)
            earlier = move_local(fetch(spacing), -before_down, -before_across).astype(jnp.float32)
            back_mask = inside_local(-before_down, -before_across) * has_before
            back_resid = back_mask * (earlier - values)
            back = back_resid / jnp.sqrt(back_resid * back_resid + charb_eps2)
            combined = combined + (scaled - back)
        total = lax.psum(energy, ("sec", "tile"))
        factor = step_size / (1.0 + total / count.astype(jnp.float32))
        field_ext = with_halo(current, (("tile", 1),), 1)
        col_pad = jnp.pad(current, ((0, 0), (0, 0), (1, 1)))
        neighbours = field_ext[:, 2:] + field_ext[:, :-2] + (col_pad[:, :, 2:] + col_pad[:, :, :-2])
        data_term = jnp.stack([combined * grad_rows, combined * grad_cols], axis=0)
        current = current - factor * (data_term + smooth_weight * (4.0 * current - neighbours))
    return current[None]


def solution(mesh):
    return jax.shard_map(
        per_device,
        mesh=mesh,
        in_specs=(P("sec", "tile", None), P("sec", None, "tile", None), P()),
        out_specs=P("sec", None, "tile", None),
        check_vma=False,
    )
```

profile of v0, /device:TPU:0, one launch (start us, length us, event | category | flops | bytes accessed | tf_op | source)
XLA Modules:
  0.0 408.2 jit_solution(16903402960520842841)
XLA Ops:
  0.7 2.4 collective-permute-start
  7.0 4.2 %collective-permute-start.15 = (f32[2,1,384]{2,1,0:T(1,128)}, f32[2,1,384]{2,1,0:T(1,128)}, u32[]{:S(2)}, u32[]{:S(2)}) collective-permute-start(f32[2,1,384]{2,1,0:T(1,128)} %get-tuple-element.51), channel_id=1, source_target_pairs={{0,1},{2,3},{4,5},{6,7},{8,9},{10,11},{12,13},{14,15},{16,17},{18,... | collective-permute-start | bytes 9224 | tf_op jit(solution)/shard_map/ppermute | solution.py:22
  68.5 4.9 %collective-permute-start.8 = (bf16[256,384]{1,0:T(8,128)(2,1)S(1)}, bf16[256,384]{1,0:T(8,128)(2,1)S(1)}, u32[]{:S(2)}, u32[]{:S(2)}) collective-permute-start(bf16[256,384]{1,0:T(8,128)(2,1)S(1)} %get-tuple-element.41), channel_id=1, source_target_pairs={{0,2},{2,4},{4,6},{6,8},{8,10},{10,12},{12,14},{14,16},{16,18},{18... | collective-permute-start | bytes 589832 | tf_op jit(solution)/shard_map/ppermute | solution.py:31
  73.4 4.6 %collective-permute-start.11 = (bf16[256,384]{1,0:T(8,128)(2,1)S(1)}, bf16[256,384]{1,0:T(8,128)(2,1)S(1)}, u32[]{:S(2)}, u32[]{:S(2)}) collective-permute-start(bf16[256,384]{1,0:T(8,128)(2,1)S(1)} %get-tuple-element.41), channel_id=1, source_target_pairs={{0,4},{2,6},{4,8},{6,10},{8,12},{10,14},{12,16},{14,18},{16,20},{1... | collective-permute-start | bytes 589832 | tf_op jit(solution)/shard_map/ppermute | solution.py:31
  80.7 6.0 %collective-permute-done.11 = bf16[256,384]{1,0:T(8,128)(2,1)S(1)} collective-permute-done((bf16[256,384]{1,0:T(8,128)(2,1)S(1)}, bf16[256,384]{1,0:T(8,128)(2,1)S(1)}, u32[]{:S(2)}, u32[]{:S(2)}) %collective-permute-start.11) | collective-permute-done | bytes 196640 | tf_op jit(solution)/shard_map/ppermute | solution.py:31
  86.6 1.9 collective-permute-start.6
  91.6 4.3 %collective-permute-start.9 = (bf16[128,384]{1,0:T(8,128)(2,1)S(1)}, bf16[128,384]{1,0:T(8,128)(2,1)}, u32[]{:S(2)}, u32[]{:S(2)}) collective-permute-start(bf16[128,384]{1,0:T(8,128)(2,1)S(1)} %get-tuple-element.79), channel_id=1, source_target_pairs={{0,1},{2,3},{4,5},{6,7},{8,9},{10,11},{12,13},{14,15},{16,17},{18,... | collective-permute-start | bytes 294920 | tf_op jit(solution)/shard_map/ppermute | solution.py:22
  95.9 1.9 collective-permute-start.12
  102.2 1.6 collective-permute-done.13
  105.6 43.6 %psum.28 = f32[]{:T(128)} all-reduce(f32[]{:T(128)S(6)} %add.927), channel_id=1, replica_groups=mesh['sec'=16,'tile'=2] {'sec','tile'}, use_global_device_ids=true, to_apply=%region_2.3 | all-reduce | flops 1 | bytes 8 | tf_op jit(solution)/shard_map/psum | solution.py:103
  153.9 4.8 %collective-permute-start.22 = (bf16[256,384]{1,0:T(8,128)(2,1)S(1)}, bf16[256,384]{1,0:T(8,128)(2,1)S(1)}, u32[]{:S(2)}, u32[]{:S(2)}) collective-permute-start(bf16[256,384]{1,0:T(8,128)(2,1)S(1)} %fusion.63), channel_id=1, source_target_pairs={{0,2},{2,4},{4,6},{6,8},{8,10},{10,12},{12,14},{14,16},{16,18},{18... | collective-permute-start | bytes 589832 | tf_op jit(solution)/shard_map/ppermute | solution.py:31
  158.7 4.8 %collective-permute-start.25 = (bf16[256,384]{1,0:T(8,128)(2,1)S(1)}, bf16[256,384]{1,0:T(8,128)(2,1)S(1)}, u32[]{:S(2)}, u32[]{:S(2)}) collective-permute-start(bf16[256,384]{1,0:T(8,128)(2,1)S(1)} %fusion.63), channel_id=1, source_target_pairs={{0,4},{2,6},{4,8},{6,10},{8,12},{10,14},{12,16},{14,18},{16,20},{1... | collective-permute-start | bytes 589832 | tf_op jit(solution)/shard_map/ppermute | solution.py:31
  165.4 4.2 %collective-permute-start.29 = (f32[2,1,384]{2,1,0:T(1,128)}, f32[2,1,384]{2,1,0:T(1,128)}, u32[]{:S(2)}, u32[]{:S(2)}) collective-permute-start(f32[2,1,384]{2,1,0:T(1,128)} %get-tuple-element.49), channel_id=1, source_target_pairs={{0,1},{2,3},{4,5},{6,7},{8,9},{10,11},{12,13},{14,15},{16,17},{18,... | collective-permute-start | bytes 9224 | tf_op jit(solution)/shard_map/ppermute | solution.py:22
  172.3 3.0 collective-permute-start.20
  176.7 3.7 collective-permute-start.23
  182.1 4.3 %collective-permute-start.26 = (bf16[128,384]{1,0:T(8,128)(2,1)S(1)}, bf16[128,384]{1,0:T(8,128)(2,1)}, u32[]{:S(2)}, u32[]{:S(2)}) collective-permute-start(bf16[128,384]{1,0:T(8,128)(2,1)S(1)} %get-tuple-element.75), channel_id=1, source_target_pairs={{0,1},{2,3},{4,5},{6,7},{8,9},{10,11},{12,13},{14,15},{16,17},{18,... | collective-permute-start | bytes 294920 | tf_op jit(solution)/shard_map/ppermute | solution.py:22
  193.5 42.5 %psum.29 = f32[]{:T(128)} all-reduce(f32[]{:T(128)S(6)} %add.975), channel_id=1, replica_groups=mesh['sec'=16,'tile'=2] {'sec','tile'}, use_global_device_ids=true, to_apply=%region_7.8 | all-reduce | flops 1 | bytes 8 | tf_op jit(solution)/shard_map/psum | solution.py:103
  240.6 4.8 %collective-permute-start.36 = (bf16[256,384]{1,0:T(8,128)(2,1)S(1)}, bf16[256,384]{1,0:T(8,128)(2,1)S(1)}, u32[]{:S(2)}, u32[]{:S(2)}) collective-permute-start(bf16[256,384]{1,0:T(8,128)(2,1)S(1)} %fusion.58), channel_id=1, source_target_pairs={{0,2},{2,4},{4,6},{6,8},{8,10},{10,12},{12,14},{14,16},{16,18},{18... | collective-permute-start | bytes 589832 | tf_op jit(solution)/shard_map/ppermute | solution.py:31
  245.4 4.8 %collective-permute-start.39 = (bf16[256,384]{1,0:T(8,128)(2,1)S(1)}, bf16[256,384]{1,0:T(8,128)(2,1)S(1)}, u32[]{:S(2)}, u32[]{:S(2)}) collective-permute-start(bf16[256,384]{1,0:T(8,128)(2,1)S(1)} %fusion.58), channel_id=1, source_target_pairs={{0,4},{2,6},{4,8},{6,10},{8,12},{10,14},{12,16},{14,18},{16,20},{1... | collective-permute-start | bytes 589832 | tf_op jit(solution)/shard_map/ppermute | solution.py:31
  252.1 4.2 %collective-permute-start.43 = (f32[2,1,384]{2,1,0:T(1,128)}, f32[2,1,384]{2,1,0:T(1,128)}, u32[]{:S(2)}, u32[]{:S(2)}) collective-permute-start(f32[2,1,384]{2,1,0:T(1,128)} %get-tuple-element.47), channel_id=1, source_target_pairs={{0,1},{2,3},{4,5},{6,7},{8,9},{10,11},{12,13},{14,15},{16,17},{18,... | collective-permute-start | bytes 9224 | tf_op jit(solution)/shard_map/ppermute | solution.py:22
  259.1 3.0 collective-permute-start.34
  263.4 3.7 collective-permute-start.37
  268.9 4.3 %collective-permute-start.40 = (bf16[128,384]{1,0:T(8,128)(2,1)S(1)}, bf16[128,384]{1,0:T(8,128)(2,1)}, u32[]{:S(2)}, u32[]{:S(2)}) collective-permute-start(bf16[128,384]{1,0:T(8,128)(2,1)S(1)} %get-tuple-element.67), channel_id=1, source_target_pairs={{0,1},{2,3},{4,5},{6,7},{8,9},{10,11},{12,13},{14,15},{16,17},{18,... | collective-permute-start | bytes 294920 | tf_op jit(solution)/shard_map/ppermute | solution.py:22
  281.1 41.3 %psum.30 = f32[]{:T(128)} all-reduce(f32[]{:T(128)S(6)} %add.1021), channel_id=1, replica_groups=mesh['sec'=16,'tile'=2] {'sec','tile'}, use_global_device_ids=true, to_apply=%region_12.13 | all-reduce | flops 1 | bytes 8 | tf_op jit(solution)/shard_map/psum | solution.py:103
  327.0 4.8 %collective-permute-start.50 = (bf16[256,384]{1,0:T(8,128)(2,1)S(1)}, bf16[256,384]{1,0:T(8,128)(2,1)S(1)}, u32[]{:S(2)}, u32[]{:S(2)}) collective-permute-start(bf16[256,384]{1,0:T(8,128)(2,1)S(1)} %fusion.53), channel_id=1, source_target_pairs={{0,2},{2,4},{4,6},{6,8},{8,10},{10,12},{12,14},{14,16},{16,18},{18... | collective-permute-start | bytes 589832 | tf_op jit(solution)/shard_map/ppermute | solution.py:31
  331.9 4.8 %collective-permute-start.53 = (bf16[256,384]{1,0:T(8,128)(2,1)S(1)}, bf16[256,384]{1,0:T(8,128)(2,1)S(1)}, u32[]{:S(2)}, u32[]{:S(2)}) collective-permute-start(bf16[256,384]{1,0:T(8,128)(2,1)S(1)} %fusion.53), channel_id=1, source_target_pairs={{0,4},{2,6},{4,8},{6,10},{8,12},{10,14},{12,16},{14,18},{16,20},{1... | collective-permute-start | bytes 589832 | tf_op jit(solution)/shard_map/ppermute | solution.py:31
  338.0 3.0 collective-permute-start.57
  344.7 2.1 collective-permute-start.48
  348.2 3.0 collective-permute-start.51
  353.0 3.0 collective-permute-start.54
  360.6 1.4 collective-permute-done.55
  363.2 42.9 %psum.31 = f32[]{:T(128)} all-reduce(f32[]{:T(128)S(6)} %add.1067), channel_id=1, replica_groups=mesh['sec'=16,'tile'=2] {'sec','tile'}, use_global_device_ids=true, to_apply=%region_17.18 | all-reduce | flops 1 | bytes 8 | tf_op jit(solution)/shard_map/psum | solution.py:103
  (288 shorter events, 99.0 us)
Async XLA Ops:
  0.7 63.6 %collective-permute-start = (bf16[1,384]{1,0:T(2,128)(2,1)S(1)}, bf16[1,384]{1,0:T(2,128)(2,1)S(1)}, u32[]{:S(2)}, u32[]{:S(2)}) collective-permute-start(bf16[1,384]{1,0:T(2,128)(2,1)S(1)} %get-tuple-element.84), channel_id=1, source_target_pairs={{0,1},{2,3},{4,5},{6,7},{8,9},{10,11},{12,13},{14,15},{16,17},{18,... | collective-permute-start | bytes 2312 | tf_op jit(solution)/shard_map/ppermute | solution.py:22
  3.1 61.2 %collective-permute-start.1 = (bf16[1,384]{1,0:T(2,128)(2,1)S(1)}, bf16[1,384]{1,0:T(2,128)(2,1)S(1)}, u32[]{:S(2)}, u32[]{:S(2)}) collective-permute-start(bf16[1,384]{1,0:T(2,128)(2,1)S(1)} %get-tuple-element.85), channel_id=1, source_target_pairs={{1,0},{3,2},{5,4},{7,6},{9,8},{11,10},{13,12},{15,14},{17,16},{19,... | collective-permute-start | bytes 2312 | tf_op jit(solution)/shard_map/ppermute | solution.py:23
  5.8 144.2 %collective-permute-start.14 = (f32[2,1,384]{2,1,0:T(1,128)}, f32[2,1,384]{2,1,0:T(1,128)}, u32[]{:S(2)}, u32[]{:S(2)}) collective-permute-start(f32[2,1,384]{2,1,0:T(1,128)} %get-tuple-element.50), channel_id=1, source_target_pairs={{1,0},{3,2},{5,4},{7,6},{9,8},{11,10},{13,12},{15,14},{17,16},{19,... | collective-permute-start | bytes 9224 | tf_op jit(solution)/shard_map/ppermute | solution.py:23
  7.0 142.9 %collective-permute-start.15 = (f32[2,1,384]{2,1,0:T(1,128)}, f32[2,1,384]{2,1,0:T(1,128)}, u32[]{:S(2)}, u32[]{:S(2)}) collective-permute-start(f32[2,1,384]{2,1,0:T(1,128)} %get-tuple-element.51), channel_id=1, source_target_pairs={{0,1},{2,3},{4,5},{6,7},{8,9},{10,11},{12,13},{14,15},{16,17},{18,... | collective-permute-start | bytes 9224 | tf_op jit(solution)/shard_map/ppermute | solution.py:22
  67.2 10.8 %collective-permute-start.5 = (bf16[256,384]{1,0:T(8,128)(2,1)S(1)}, bf16[256,384]{1,0:T(8,128)(2,1)S(1)}, u32[]{:S(2)}, u32[]{:S(2)}) collective-permute-start(bf16[256,384]{1,0:T(8,128)(2,1)S(1)} %get-tuple-element.41), channel_id=1, source_target_pairs={{4,0},{6,2},{8,4},{10,6},{12,8},{14,10},{16,12},{18,14},{20,16},{2... | collective-permute-start | bytes 589832 | tf_op jit(solution)/shard_map/ppermute | solution.py:31
  68.5 10.8 %collective-permute-start.8 = (bf16[256,384]{1,0:T(8,128)(2,1)S(1)}, bf16[256,384]{1,0:T(8,128)(2,1)S(1)}, u32[]{:S(2)}, u32[]{:S(2)}) collective-permute-start(bf16[256,384]{1,0:T(8,128)(2,1)S(1)} %get-tuple-element.41), channel_id=1, source_target_pairs={{0,2},{2,4},{4,6},{6,8},{8,10},{10,12},{12,14},{14,16},{16,18},{18... | collective-permute-start | bytes 589832 | tf_op jit(solution)/shard_map/ppermute | solution.py:31
  73.4 13.3 %collective-permute-start.11 = (bf16[256,384]{1,0:T(8,128)(2,1)S(1)}, bf16[256,384]{1,0:T(8,128)(2,1)S(1)}, u32[]{:S(2)}, u32[]{:S(2)}) collective-permute-start(bf16[256,384]{1,0:T(8,128)(2,1)S(1)} %get-tuple-element.41), channel_id=1, source_target_pairs={{0,4},{2,6},{4,8},{6,10},{8,12},{10,14},{12,16},{14,18},{16,20},{1... | collective-permute-start | bytes 589832 | tf_op jit(solution)/shard_map/ppermute | solution.py:31
  78.0 10.6 %collective-permute-start.3 = (bf16[128,384]{1,0:T(8,128)(2,1)S(1)}, bf16[128,384]{1,0:T(8,128)(2,1)S(1)}, u32[]{:S(2)}, u32[]{:S(2)}) collective-permute-start(bf16[128,384]{1,0:T(8,128)(2,1)S(1)} %get-tuple-element.77), channel_id=1, source_target_pairs={{0,1},{2,3},{4,5},{6,7},{8,9},{10,11},{12,13},{14,15},{16,17},{18,... | collective-permute-start | bytes 294920 | tf_op jit(solution)/shard_map/ppermute | solution.py:22
  79.3 10.6 %collective-permute-start.4 = (bf16[128,384]{1,0:T(8,128)(2,1)S(1)}, bf16[128,384]{1,0:T(8,128)(2,1)S(1)}, u32[]{:S(2)}, u32[]{:S(2)}) collective-permute-start(bf16[128,384]{1,0:T(8,128)(2,1)S(1)} %get-tuple-element.76), channel_id=1, source_target_pairs={{1,0},{3,2},{5,4},{7,6},{9,8},{11,10},{13,12},{15,14},{17,16},{19,... | collective-permute-start | bytes 294920 | tf_op jit(solution)/shard_map/ppermute | solution.py:23
  89.9 10.7 %collective-permute-start.10 = (bf16[128,384]{1,0:T(8,128)(2,1)S(1)}, bf16[128,384]{1,0:T(8,128)(2,1)}, u32[]{:S(2)}, u32[]{:S(2)}) collective-permute-start(bf16[128,384]{1,0:T(8,128)(2,1)S(1)} %get-tuple-element.78), channel_id=1, source_target_pairs={{1,0},{3,2},{5,4},{7,6},{9,8},{11,10},{13,12},{15,14},{17,16},{19,... | collective-permute-start | bytes 294920 | tf_op jit(solution)/shard_map/ppermute | solution.py:23
  91.6 10.3 %collective-permute-start.9 = (bf16[128,384]{1,0:T(8,128)(2,1)S(1)}, bf16[128,384]{1,0:T(8,128)(2,1)}, u32[]{:S(2)}, u32[]{:S(2)}) collective-permute-start(bf16[128,384]{1,0:T(8,128)(2,1)S(1)} %get-tuple-element.79), channel_id=1, source_target_pairs={{0,1},{2,3},{4,5},{6,7},{8,9},{10,11},{12,13},{14,15},{16,17},{18,... | collective-permute-start | bytes 294920 | tf_op jit(solution)/shard_map/ppermute | solution.py:22
  151.3 14.1 %collective-permute-start.16 = (bf16[256,384]{1,0:T(8,128)(2,1)S(1)}, bf16[256,384]{1,0:T(8,128)(2,1)S(1)}, u32[]{:S(2)}, u32[]{:S(2)}) collective-permute-start(bf16[256,384]{1,0:T(8,128)(2,1)S(1)} %fusion.63), channel_id=1, source_target_pairs={{2,0},{4,2},{6,4},{8,6},{10,8},{12,10},{14,12},{16,14},{18,16},{20... | collective-permute-start | bytes 589832 | tf_op jit(solution)/shard_map/ppermute | solution.py:31
  152.6 17.1 %collective-permute-start.19 = (bf16[256,384]{1,0:T(8,128)(2,1)S(1)}, bf16[256,384]{1,0:T(8,128)(2,1)S(1)}, u32[]{:S(2)}, u32[]{:S(2)}) collective-permute-start(bf16[256,384]{1,0:T(8,128)(2,1)S(1)} %fusion.63), channel_id=1, source_target_pairs={{4,0},{6,2},{8,4},{10,6},{12,8},{14,10},{16,12},{18,14},{20,16},{2... | collective-permute-start | bytes 589832 | tf_op jit(solution)/shard_map/ppermute | solution.py:31
  153.9 17.1 %collective-permute-start.22 = (bf16[256,384]{1,0:T(8,128)(2,1)S(1)}, bf16[256,384]{1,0:T(8,128)(2,1)S(1)}, u32[]{:S(2)}, u32[]{:S(2)}) collective-permute-start(bf16[256,384]{1,0:T(8,128)(2,1)S(1)} %fusion.63), channel_id=1, source_target_pairs={{0,2},{2,4},{4,6},{6,8},{8,10},{10,12},{12,14},{14,16},{16,18},{18... | collective-permute-start | bytes 589832 | tf_op jit(solution)/shard_map/ppermute | solution.py:31
  158.7 13.6 %collective-permute-start.25 = (bf16[256,384]{1,0:T(8,128)(2,1)S(1)}, bf16[256,384]{1,0:T(8,128)(2,1)S(1)}, u32[]{:S(2)}, u32[]{:S(2)}) collective-permute-start(bf16[256,384]{1,0:T(8,128)(2,1)S(1)} %fusion.63), channel_id=1, source_target_pairs={{0,4},{2,6},{4,8},{6,10},{8,12},{10,14},{12,16},{14,18},{16,20},{1... | collective-permute-start | bytes 589832 | tf_op jit(solution)/shard_map/ppermute | solution.py:31
  164.1 72.6 %collective-permute-start.28 = (f32[2,1,384]{2,1,0:T(1,128)}, f32[2,1,384]{2,1,0:T(1,128)}, u32[]{:S(2)}, u32[]{:S(2)}) collective-permute-start(f32[2,1,384]{2,1,0:T(1,128)} %get-tuple-element.48), channel_id=1, source_target_pairs={{1,0},{3,2},{5,4},{7,6},{9,8},{11,10},{13,12},{15,14},{17,16},{19,... | collective-permute-start | bytes 9224 | tf_op jit(solution)/shard_map/ppermute | solution.py:23
  165.4 71.3 %collective-permute-start.29 = (f32[2,1,384]{2,1,0:T(1,128)}, f32[2,1,384]{2,1,0:T(1,128)}, u32[]{:S(2)}, u32[]{:S(2)}) collective-permute-start(f32[2,1,384]{2,1,0:T(1,128)} %get-tuple-element.49), channel_id=1, source_target_pairs={{0,1},{2,3},{4,5},{6,7},{8,9},{10,11},{12,13},{14,15},{16,17},{18,... | collective-permute-start | bytes 9224 | tf_op jit(solution)/shard_map/ppermute | solution.py:22
  176.7 12.5 %collective-permute-start.23 = (bf16[128,384]{1,0:T(8,128)(2,1)S(1)}, bf16[128,384]{1,0:T(8,128)(2,1)}, u32[]{:S(2)}, u32[]{:S(2)}) collective-permute-start(bf16[128,384]{1,0:T(8,128)(2,1)S(1)} %get-tuple-element.71), channel_id=1, source_target_pairs={{0,1},{2,3},{4,5},{6,7},{8,9},{10,11},{12,13},{14,15},{16,17},{18,... | collective-permute-start | bytes 294920 | tf_op jit(solution)/shard_map/ppermute | solution.py:22
  238.0 14.1 %collective-permute-start.30 = (bf16[256,384]{1,0:T(8,128)(2,1)S(1)}, bf16[256,384]{1,0:T(8,128)(2,1)S(1)}, u32[]{:S(2)}, u32[]{:S(2)}) collective-permute-start(bf16[256,384]{1,0:T(8,128)(2,1)S(1)} %fusion.58), channel_id=1, source_target_pairs={{2,0},{4,2},{6,4},{8,6},{10,8},{12,10},{14,12},{16,14},{18,16},{20... | collective-permute-start | bytes 589832 | tf_op jit(solution)/shard_map/ppermute | solution.py:31
  239.3 17.0 %collective-permute-start.33 = (bf16[256,384]{1,0:T(8,128)(2,1)S(1)}, bf16[256,384]{1,0:T(8,128)(2,1)S(1)}, u32[]{:S(2)}, u32[]{:S(2)}) collective-permute-start(bf16[256,384]{1,0:T(8,128)(2,1)S(1)} %fusion.58), channel_id=1, source_target_pairs={{4,0},{6,2},{8,4},{10,6},{12,8},{14,10},{16,12},{18,14},{20,16},{2... | collective-permute-start | bytes 589832 | tf_op jit(solution)/shard_map/ppermute | solution.py:31
  240.6 17.1 %collective-permute-start.36 = (bf16[256,384]{1,0:T(8,128)(2,1)S(1)}, bf16[256,384]{1,0:T(8,128)(2,1)S(1)}, u32[]{:S(2)}, u32[]{:S(2)}) collective-permute-start(bf16[256,384]{1,0:T(8,128)(2,1)S(1)} %fusion.58), channel_id=1, source_target_pairs={{0,2},{2,4},{4,6},{6,8},{8,10},{10,12},{12,14},{14,16},{16,18},{18... | collective-permute-start | bytes 589832 | tf_op jit(solution)/shard_map/ppermute | solution.py:31
  245.4 13.6 %collective-permute-start.39 = (bf16[256,384]{1,0:T(8,128)(2,1)S(1)}, bf16[256,384]{1,0:T(8,128)(2,1)S(1)}, u32[]{:S(2)}, u32[]{:S(2)}) collective-permute-start(bf16[256,384]{1,0:T(8,128)(2,1)S(1)} %fusion.58), channel_id=1, source_target_pairs={{0,4},{2,6},{4,8},{6,10},{8,12},{10,14},{12,16},{14,18},{16,20},{1... | collective-permute-start | bytes 589832 | tf_op jit(solution)/shard_map/ppermute | solution.py:31
  250.8 72.3 %collective-permute-start.42 = (f32[2,1,384]{2,1,0:T(1,128)}, f32[2,1,384]{2,1,0:T(1,128)}, u32[]{:S(2)}, u32[]{:S(2)}) collective-permute-start(f32[2,1,384]{2,1,0:T(1,128)} %get-tuple-element.46), channel_id=1, source_target_pairs={{1,0},{3,2},{5,4},{7,6},{9,8},{11,10},{13,12},{15,14},{17,16},{19,... | collective-permute-start | bytes 9224 | tf_op jit(solution)/shard_map/ppermute | solution.py:23
  252.1 71.0 %collective-permute-start.43 = (f32[2,1,384]{2,1,0:T(1,128)}, f32[2,1,384]{2,1,0:T(1,128)}, u32[]{:S(2)}, u32[]{:S(2)}) collective-permute-start(f32[2,1,384]{2,1,0:T(1,128)} %get-tuple-element.47), channel_id=1, source_target_pairs={{0,1},{2,3},{4,5},{6,7},{8,9},{10,11},{12,13},{14,15},{16,17},{18,... | collective-permute-start | bytes 9224 | tf_op jit(solution)/shard_map/ppermute | solution.py:22
  263.4 12.4 %collective-permute-start.37 = (bf16[128,384]{1,0:T(8,128)(2,1)S(1)}, bf16[128,384]{1,0:T(8,128)(2,1)}, u32[]{:S(2)}, u32[]{:S(2)}) collective-permute-start(bf16[128,384]{1,0:T(8,128)(2,1)S(1)} %get-tuple-element.63), channel_id=1, source_target_pairs={{0,1},{2,3},{4,5},{6,7},{8,9},{10,11},{12,13},{14,15},{16,17},{18,... | collective-permute-start | bytes 294920 | tf_op jit(solution)/shard_map/ppermute | solution.py:22
  324.4 13.6 %collective-permute-start.44 = (bf16[256,384]{1,0:T(8,128)(2,1)S(1)}, bf16[256,384]{1,0:T(8,128)(2,1)S(1)}, u32[]{:S(2)}, u32[]{:S(2)}) collective-permute-start(bf16[256,384]{1,0:T(8,128)(2,1)S(1)} %fusion.53), channel_id=1, source_target_pairs={{2,0},{4,2},{6,4},{8,6},{10,8},{12,10},{14,12},{16,14},{18,16},{20... | collective-permute-start | bytes 589832 | tf_op jit(solution)/shard_map/ppermute | solution.py:31
  325.7 15.3 %collective-permute-start.47 = (bf16[256,384]{1,0:T(8,128)(2,1)S(1)}, bf16[256,384]{1,0:T(8,128)(2,1)S(1)}, u32[]{:S(2)}, u32[]{:S(2)}) collective-permute-start(bf16[256,384]{1,0:T(8,128)(2,1)S(1)} %fusion.53), channel_id=1, source_target_pairs={{4,0},{6,2},{8,4},{10,6},{12,8},{14,10},{16,12},{18,14},{20,16},{2... | collective-permute-start | bytes 589832 | tf_op jit(solution)/shard_map/ppermute | solution.py:31
  327.0 15.4 %collective-permute-start.50 = (bf16[256,384]{1,0:T(8,128)(2,1)S(1)}, bf16[256,384]{1,0:T(8,128)(2,1)S(1)}, u32[]{:S(2)}, u32[]{:S(2)}) collective-permute-start(bf16[256,384]{1,0:T(8,128)(2,1)S(1)} %fusion.53), channel_id=1, source_target_pairs={{0,2},{2,4},{4,6},{6,8},{8,10},{10,12},{12,14},{14,16},{16,18},{18... | collective-permute-start | bytes 589832 | tf_op jit(solution)/shard_map/ppermute | solution.py:31
  331.9 12.9 %collective-permute-start.53 = (bf16[256,384]{1,0:T(8,128)(2,1)S(1)}, bf16[256,384]{1,0:T(8,128)(2,1)S(1)}, u32[]{:S(2)}, u32[]{:S(2)}) collective-permute-start(bf16[256,384]{1,0:T(8,128)(2,1)S(1)} %fusion.53), channel_id=1, source_target_pairs={{0,4},{2,6},{4,8},{6,10},{8,12},{10,14},{12,16},{14,18},{16,20},{1... | collective-permute-start | bytes 589832 | tf_op jit(solution)/shard_map/ppermute | solution.py:31
  336.7 70.1 %collective-permute-start.56 = (f32[2,1,384]{2,1,0:T(1,128)S(1)}, f32[2,1,384]{2,1,0:T(1,128)S(1)}, u32[]{:S(2)}, u32[]{:S(2)}) collective-permute-start(f32[2,1,384]{2,1,0:T(1,128)S(1)} %get-tuple-element.44), channel_id=1, source_target_pairs={{1,0},{3,2},{5,4},{7,6},{9,8},{11,10},{13,12},{15,14},{17,16},{19,... | collective-permute-start | bytes 9224 | tf_op jit(solution)/shard_map/ppermute | solution.py:23
  338.0 68.8 %collective-permute-start.57 = (f32[2,1,384]{2,1,0:T(1,128)S(1)}, f32[2,1,384]{2,1,0:T(1,128)S(1)}, u32[]{:S(2)}, u32[]{:S(2)}) collective-permute-start(f32[2,1,384]{2,1,0:T(1,128)S(1)} %get-tuple-element.45), channel_id=1, source_target_pairs={{0,1},{2,3},{4,5},{6,7},{8,9},{10,11},{12,13},{14,15},{16,17},{18,... | collective-permute-start | bytes 9224 | tf_op jit(solution)/shard_map/ppermute | solution.py:22
  348.2 10.7 %collective-permute-start.51 = (bf16[128,384]{1,0:T(8,128)(2,1)S(1)}, bf16[128,384]{1,0:T(8,128)(2,1)S(1)}, u32[]{:S(2)}, u32[]{:S(2)}) collective-permute-start(bf16[128,384]{1,0:T(8,128)(2,1)S(1)} %get-tuple-element.55), channel_id=1, source_target_pairs={{0,1},{2,3},{4,5},{6,7},{8,9},{10,11},{12,13},{14,15},{16,17},{18,... | collective-permute-start | bytes 294920 | tf_op jit(solution)/shard_map/ppermute | solution.py:22
  (72 other events, 302.1 us)
where the time goes:
time: 411 us; the launch traced here: 408 us
  blocking collectives  170 us (41%)
  starting transfers between devices  137 us (33%)
  other arithmetic  40.5 us (10%)
  between operations  35.2 us (9%)
  local copies, waits for them, and re-layouts  13.4 us (3%)
  waiting for transfers between devices  11.5 us (3%)
    psum x4, blocking collectives, per_device(): total = lax.psum(energy, ('sec', 'tile'))  170 us
    ppermute x21, starting transfers between devices, with_halo(): before = lax.ppermute(last, axis, up)  61.4 us
    ppermute x16, starting transfers between devices, passed_along(): lax.ppermute(value, axis, [(source, source + steps) for source in range(l...  48.7 us
    ppermute x21, starting transfers between devices, with_halo(): after = lax.ppermute(leading, axis, down)  27.1 us
    convert_element_type x16, other arithmetic, inside_local(): good_rows = ((row_pos >= 0) & (row_pos < height)).astype(jnp.float32)  9.24 us
    convert_element_type x16, other arithmetic, inside_local(): good_cols = ((col_pos >= 0) & (col_pos < width)).astype(jnp.float32)  8.79 us
    concatenate x16, other arithmetic, with_halo(): shard = jnp.concatenate([before, shard, after], axis=dim)  8.49 us
  transfers between devices with their start and end apart: 58, of which 6 were waited for; matrix products, arithmetic and copies ran while one was open for 11% of the time, Pallas kernels for 0%

commit v1 on v0

v1 whole, which is shorter than its diff:
```python
import functools

import jax
import jax.numpy as jnp
from jax import lax
from jax.experimental import pallas as pl
from jax.experimental.pallas import tpu as pltpu
from jax.sharding import PartitionSpec as P

BLOCK = 128
ITERS = 4
CHUNK = 32
PAD = 8
OFFSETS = (1, 2, -1, -2)

charb_eps2 = 0.25
step_size = 0.2
smooth_weight = 0.5

MESH = pl.DeviceIdType.MESH


def kernel(sections, tiles, image_ref, field_ref, disp_ref, out_ref, *scratch):
    moved_refs = (scratch[0:4], scratch[4:8])
    (warp_ref, u_ref, img_ref, grow_ref, gcol_ref, comb_ref, data_ref, own_ref, sum_ref, tile_slots, sec_slots) = scratch[8:19]
    (img_send, img_recv, u_send, u_recv, w_send, w_recv, h_send, h_recv, t_send, t_recv, s_send, s_recv) = scratch[19:]
    rows, width = grow_ref.shape
    height = rows * tiles
    cols = width // BLOCK
    chunks = rows // CHUNK
    section = lax.axis_index("sec")
    tile = lax.axis_index("tile")

    barrier = pltpu.get_barrier_semaphore()
    for d in range(1, sections):
        pl.semaphore_signal(barrier, inc=1, device_id=(lax.rem(section + d, sections), tile), device_id_type=MESH)
    for d in range(1, tiles):
        pl.semaphore_signal(barrier, inc=1, device_id=(section, lax.rem(tile + d, tiles)), device_id_type=MESH)

    def remote(src, dst, send, recv, sec_at, tile_at):
        return pltpu.make_async_remote_copy(
            src_ref=src, dst_ref=dst, send_sem=send, recv_sem=recv, device_id=(sec_at, tile_at), device_id_type=MESH
        )

    has_above = tile > 0
    has_below = tile < tiles - 1
    above = jnp.maximum(tile - 1, 0)
    below = jnp.minimum(tile + 1, tiles - 1)

    def edge_copies(ref, send, recv):
        up = remote(ref.at[..., pl.ds(PAD, PAD), :], ref.at[..., pl.ds(rows + PAD, PAD), :], send.at[0], recv.at[0], section, above)
        down = remote(ref.at[..., pl.ds(rows, PAD), :], ref.at[..., pl.ds(0, PAD), :], send.at[1], recv.at[1], section, below)
        return up, down

    def edge_start(ref, send, recv):
        up, down = edge_copies(ref, send, recv)
        pl.when(has_above)(up.start)
        pl.when(has_below)(down.start)

    def edge_wait(ref, send, recv):
        up, down = edge_copies(ref, send, recv)
        pl.when(has_below)(up.wait_recv)
        pl.when(has_above)(down.wait_recv)
        pl.when(has_above)(up.wait_send)
        pl.when(has_below)(down.wait_send)

    @pl.when(jnp.logical_not(has_above))
    def _():
        img_ref[0:PAD, :] = jnp.zeros((PAD, width), jnp.float32)
        for p in range(2):
            u_ref[p, :, 0:PAD, :] = jnp.zeros((2, PAD, width), jnp.float32)

    @pl.when(jnp.logical_not(has_below))
    def _():
        img_ref[rows + PAD : rows + 2 * PAD, :] = jnp.zeros((PAD, width), jnp.float32)
        for p in range(2):
            u_ref[p, :, rows + PAD : rows + 2 * PAD, :] = jnp.zeros((2, PAD, width), jnp.float32)

    def chunk_loop(body, init=None):
        def step(c, carry):
            return body(c, pl.multiple_of(c * CHUNK, CHUNK), carry)

        return lax.fori_loop(0, chunks, step, init)

    def load_in(c, r, carry):
        img_ref[pl.ds(r + PAD, CHUNK), :] = image_ref[0, pl.ds(r, CHUNK), :].astype(jnp.float32)
        u_ref[0, :, pl.ds(r + PAD, CHUNK), :] = field_ref[0, :, pl.ds(r, CHUNK), :]
        return carry

    chunk_loop(load_in, 0)

    pl.semaphore_wait(barrier, sections - 1 + tiles - 1)
    edge_start(img_ref, img_send, img_recv)
    edge_wait(img_ref, img_send, img_recv)

    def block_of(c):
        block = c // (BLOCK // CHUNK)
        return block, pl.multiple_of((c - block * (BLOCK // CHUNK)) * CHUNK, CHUNK)

    col_ids = lax.broadcasted_iota(jnp.int32, (CHUNK, width), 1)

    def left_right(x):
        left = jnp.where(col_ids == 0, 0.0, pltpu.roll(x, 1, 1))
        right = jnp.where(col_ids == width - 1, 0.0, pltpu.roll(x, width - 1, 1))
        return left, right

    def store_warp(p, c, base, grow, gcol, u0, u1):
        warped = (base + grow * u0 + gcol * u1).astype(jnp.bfloat16)
        block, sub = block_of(c)
        for j in range(cols):
            warp_ref[p, block, j, pl.ds(sub, CHUNK), :] = warped[:, j * BLOCK : (j + 1) * BLOCK]

    def first_warp(c, r, carry):
        band = img_ref[pl.ds(r, CHUNK + 2 * PAD), :]
        base = band[PAD : PAD + CHUNK]
        grow = 0.5 * (band[PAD + 1 : PAD + 1 + CHUNK] - band[PAD - 1 : PAD - 1 + CHUNK])
        left, right = left_right(base)
        gcol = 0.5 * (right - left)
        grow_ref[pl.ds(r, CHUNK), :] = grow
        gcol_ref[pl.ds(r, CHUNK), :] = gcol
        u0 = u_ref[0, 0, pl.ds(r + PAD, CHUNK), :]
        u1 = u_ref[0, 1, pl.ds(r + PAD, CHUNK), :]
        store_warp(0, c, base, grow, gcol, u0, u1)
        return carry

    chunk_loop(first_warp, 0)

    def in_stack(at):
        return (at >= 0) & (at < sections)

    def step(turn, p):
        refs = moved_refs[p]

        def main_copy(i):
            target = jnp.clip(section - OFFSETS[i], 0, sections - 1)
            return remote(
                warp_ref.at[p], refs[i].at[pl.ds(1, rows // BLOCK)], w_send.at[p, i], w_recv.at[p, i], target, tile
            )

        def relay_up(i):
            return remote(
                refs[i].at[1], refs[i].at[rows // BLOCK + 1],
                h_send.at[p, i, 0], h_recv.at[p, i, 0], section, above,
            )

        def relay_down(i):
            return remote(
                refs[i].at[rows // BLOCK], refs[i].at[0],
                h_send.at[p, i, 1], h_recv.at[p, i, 1], section, below,
            )

        def start_main(i):
            pl.when(in_stack(section - OFFSETS[i]))(main_copy(i).start)

        def relay(i):
            @pl.when(in_stack(section + OFFSETS[i]))
            def _():
                main_copy(i).wait_recv()
                pl.when(has_above)(relay_up(i).start)
                pl.when(has_below)(relay_down(i).start)

        def arrive(i):
            @pl.when(in_stack(section + OFFSETS[i]))
            def _():
                pl.when(has_below)(relay_up(i).wait_recv)
                pl.when(has_above)(relay_down(i).wait_recv)

        def finish(i):
            pl.when(in_stack(section - OFFSETS[i]))(main_copy(i).wait_send)

            @pl.when(in_stack(section + OFFSETS[i]))
            def _():
                pl.when(has_above)(relay_up(i).wait_send)
                pl.when(has_below)(relay_down(i).wait_send)

        for i in range(4):
            start_main(i)
        edge_start(u_ref.at[p], u_send.at[p], u_recv.at[p])

        def count_one(s, total):
            for g in (1, 2):
                at = ((turn * sections + s) * 2 + (g - 1)) * 2
                area = (height - BLOCK * jnp.abs(disp_ref[at])) * (width - BLOCK * jnp.abs(disp_ref[at + 1]))
                total = total + (s + g < sections).astype(jnp.int32) * area
            return total

        count = lax.fori_loop(0, sections, count_one, jnp.int32(0))

        def shift_of(i):
            g = abs(OFFSETS[i])
            first = section if OFFSETS[i] > 0 else jnp.maximum(section - g, 0)
            sign = 1 if OFFSETS[i] > 0 else -1
            at = ((turn * sections + first) * 2 + (g - 1)) * 2
            return sign * disp_ref[at], sign * disp_ref[at + 1]

        def residual(i, c, r, j, own, down, across):
            block, sub = block_of(c)
            row_block = tile * (rows // BLOCK) + block + down
            col_block = j + across
            good = in_stack(section + OFFSETS[i]) & (row_block >= 0) & (row_block < height // BLOCK)
            good = good & (col_block >= 0) & (col_block < cols)
            other = refs[i][block + 1 + down, jnp.minimum(jnp.maximum(col_block, 0), cols - 1), pl.ds(sub, CHUNK), :].astype(jnp.float32)
            mask = jnp.full((CHUNK, BLOCK), good.astype(jnp.int32), jnp.int32)
            resid = jnp.where(mask > 0, own - other, 0.0)
            return resid, resid * lax.rsqrt(resid * resid + charb_eps2)

        relay(0)
        relay(1)
        arrive(0)
        arrive(1)
        shifts = [shift_of(i) for i in range(4)]

        def forward(c, r, energy):
            block, sub = block_of(c)
            for j in range(cols):
                own = warp_ref[p, block, j, pl.ds(sub, CHUNK), :].astype(jnp.float32)
                resid_a, scaled_a = residual(0, c, r, j, own, *shifts[0])
                resid_b, scaled_b = residual(1, c, r, j, own, *shifts[1])
                energy = energy + (resid_a * scaled_a + resid_b * scaled_b)
                comb_ref[pl.ds(r, CHUNK), j * BLOCK : (j + 1) * BLOCK] = scaled_a + scaled_b
            return energy

        energy = chunk_loop(forward, jnp.zeros((CHUNK, BLOCK), jnp.float32))
        own_ref[p] = jnp.sum(energy.reshape(CHUNK // 8, 8, BLOCK), axis=0)

        def tile_copy(d):
            return remote(own_ref.at[p], tile_slots.at[p, d - 1], t_send.at[p, d - 1], t_recv.at[p, d - 1], section, lax.rem(tile + d, tiles))

        def sec_copy(d):
            return remote(sum_ref.at[p], sec_slots.at[p, d - 1], s_send.at[p, d - 1], s_recv.at[p, d - 1], lax.rem(section + d, sections), tile)

        for d in range(1, tiles):
            tile_copy(d).start()
        relay(2)
        relay(3)
        total = own_ref[p]
        for d in range(1, tiles):
            tile_copy(d).wait_recv()
            total = total + tile_slots[p, d - 1]
        sum_ref[p] = total
        for d in range(1, sections):
            sec_copy(d).start()
        arrive(2)
        arrive(3)
        edge_wait(u_ref.at[p], u_send.at[p], u_recv.at[p])

        def backward(c, r, carry):
            block, sub = block_of(c)
            parts = []
            for j in range(cols):
                own = warp_ref[p, block, j, pl.ds(sub, CHUNK), :].astype(jnp.float32)
                _, scaled_a = residual(2, c, r, j, own, *shifts[2])
                _, scaled_b = residual(3, c, r, j, own, *shifts[3])
                parts.append(comb_ref[pl.ds(r, CHUNK), j * BLOCK : (j + 1) * BLOCK] + (scaled_a + scaled_b))
            combined = jnp.concatenate(parts, axis=1)
            for n, grad_ref in enumerate((grow_ref, gcol_ref)):
                band = u_ref[p, n, pl.ds(r, CHUNK + 2 * PAD), :]
                here = band[PAD : PAD + CHUNK]
                left, right = left_right(here)
                around = band[PAD + 1 : PAD + 1 + CHUNK] + band[PAD - 1 : PAD - 1 + CHUNK] + (right + left)
                data_ref[n, pl.ds(r, CHUNK), :] = combined * grad_ref[pl.ds(r, CHUNK), :] + smooth_weight * (4.0 * here - around)
            return carry

        chunk_loop(backward, 0)

        for i in range(4):
            finish(i)
        total = sum_ref[p]
        for d in range(1, sections):
            sec_copy(d).wait_recv()
            total = total + sec_slots[p, d - 1]
        energy_all = jnp.sum(jnp.sum(total, axis=0, keepdims=True), axis=1, keepdims=True)
        count_all = jnp.full((1, 1), count, jnp.int32).astype(jnp.float32)
        factor = step_size / (1.0 + energy_all / count_all)
        for d in range(1, tiles):
            tile_copy(d).wait_send()
        for d in range(1, sections):
            sec_copy(d).wait_send()

        def update(c, r, carry):
            news = []
            for n in range(2):
                new = u_ref[p, n, pl.ds(r + PAD, CHUNK), :] - factor * data_ref[n, pl.ds(r, CHUNK), :]
                u_ref[1 - p, n, pl.ds(r + PAD, CHUNK), :] = new
                news.append(new)
            base = img_ref[pl.ds(r + PAD, CHUNK), :]
            store_warp(1 - p, c, base, grow_ref[pl.ds(r, CHUNK), :], gcol_ref[pl.ds(r, CHUNK), :], *news)
            return carry

        chunk_loop(update, 0)

    def two_steps(half, carry):
        step(2 * half, 0)
        step(2 * half + 1, 1)
        return carry

    lax.fori_loop(0, ITERS // 2, two_steps, 0)

    def store_out(c, r, carry):
        out_ref[0, :, pl.ds(r, CHUNK), :] = u_ref[0, :, pl.ds(r + PAD, CHUNK), :]
        return carry

    chunk_loop(store_out, 0)


def solution(mesh):
    sections, tiles = mesh.shape["sec"], mesh.shape["tile"]

    def per_device(image, field, displacement):
        rows, width = image.shape[1], image.shape[2]
        cols = width // BLOCK
        dma = pltpu.SemaphoreType.DMA
        return pl.pallas_call(
            functools.partial(kernel, sections, tiles),
            out_shape=jax.ShapeDtypeStruct(field.shape, jnp.float32),
            in_specs=[
                pl.BlockSpec(memory_space=pltpu.VMEM),
                pl.BlockSpec(memory_space=pltpu.VMEM),
                pl.BlockSpec(memory_space=pltpu.SMEM),
            ],
            out_specs=pl.BlockSpec(memory_space=pltpu.VMEM),
            scratch_shapes=[pltpu.VMEM((rows // BLOCK + 2, cols, BLOCK, BLOCK), jnp.bfloat16) for _ in range(8)]
            + [
                pltpu.VMEM((2, rows // BLOCK, cols, BLOCK, BLOCK), jnp.bfloat16),
                pltpu.VMEM((2, 2, rows + 2 * PAD, width), jnp.float32),
                pltpu.VMEM((rows + 2 * PAD, width), jnp.float32),
                pltpu.VMEM((rows, width), jnp.float32),
                pltpu.VMEM((rows, width), jnp.float32),
                pltpu.VMEM((rows, width), jnp.float32),
                pltpu.VMEM((2, rows, width), jnp.float32),
                pltpu.VMEM((2, 8, BLOCK), jnp.float32),
                pltpu.VMEM((2, 8, BLOCK), jnp.float32),
                pltpu.VMEM((2, tiles - 1, 8, BLOCK), jnp.float32),
                pltpu.VMEM((2, sections - 1, 8, BLOCK), jnp.float32),
                dma((2,)), dma((2,)),
                dma((2, 2)), dma((2, 2)),
                dma((2, 4)), dma((2, 4)),
                dma((2, 4, 2)), dma((2, 4, 2)),
                dma((2, tiles - 1)), dma((2, tiles - 1)),
                dma((2, sections - 1)), dma((2, sections - 1)),
            ],
            compiler_params=pltpu.CompilerParams(
                collective_id=0, has_side_effects=True, vmem_limit_bytes=48 * 1024 * 1024
            ),
        )(image, field, displacement.reshape(-1))

    return jax.shard_map(
        per_device,
        mesh=mesh,
        in_specs=(P("sec", "tile", None), P("sec", None, "tile", None), P()),
        out_specs=P("sec", None, "tile", None),
        check_vma=False,
    )
```

time: 411 us -> 97.9 us (0.24)
  blocking collectives: 170 us -> 0 us
  starting transfers between devices: 137 us -> 0 us
  Pallas kernels: 0 us -> 93.8 us
  other arithmetic: 40.5 us -> 0 us
  between operations: 35.2 us -> 0.02 us
  waiting for transfers between devices: 11.5 us -> 0 us
  local copies, waits for them, and re-layouts: 13.4 us -> 3.9 us
    psum x4 -> x0, blocking collectives: 170 us -> none  [per_device(): total = lax.psum(energy, ('sec', 'tile'))]
    ppermute x58 -> x0, starting transfers between devices: 137 us -> none  [the longest x21 61.4 us: with_halo(): before = lax.ppermute(last, axis, up)]
    pallas_call x0 -> x1, Pallas kernels: none -> 93.8 us  [per_device(): pl.pallas_call(functools.partial(kernel, sections, tiles), out_shape=jax....]
    convert_element_type x37 -> x0, other arithmetic: 18.7 us -> none  [the longest x16 9.24 us: inside_local(): good_rows = ((row_pos >= 0) & (row_pos < height)).astype(jnp.float32)]
    ppermute x58 -> x0, waiting for transfers between devices: 11.5 us -> none  [the longest x16 6.97 us: passed_along(): lax.ppermute(value, axis, [(source, source + steps) for source in range(l...]
    slice x34 -> x0, local copies, waits for them, and re-layouts: 11.2 us -> none  [the longest x8 4.95 us: per_device(): before_down = before_pairs[spacing - 1, 0]]
    concatenate x16 -> x0, other arithmetic: 8.49 us -> none  [with_halo(): shard = jnp.concatenate([before, shard, after], axis=dim)]
    reduce_sum x6 -> x0, other arithmetic: 5.74 us -> none  [the longest x4 4.26 us: per_device(): energy = energy + jnp.sum(scaled * resid)]
  transfers between devices with their start and end apart: 58 -> 0, of which waited for: 6 -> 0; matrix products, arithmetic and copies ran while one was open for 11% -> 0% of each run, Pallas kernels for 0% -> 0%
where the time goes in v1:
time: 97.9 us; the launch traced here: 97.7 us
  Pallas kernels  93.8 us (96%)
  local copies, waits for them, and re-layouts  3.9 us (4%)
    pallas_call x1, Pallas kernels, per_device(): pl.pallas_call(functools.partial(kernel, sections, tiles), out_shape=jax....  93.8 us
    unnamed x6, local copies, waits for them, and re-layouts  3.76 us

profile of v1, /device:TPU:0, one launch (start us, length us, event | category | flops | bytes accessed | tf_op | source)
XLA Modules:
  0.0 97.7 jit_solution(6003808031904851216)
XLA Ops:
  0.0 0.8 copy.4
  0.8 0.1 reshape.3.disp_ref
  1.0 0.0 copy-start
  1.0 1.1 %copy-done = f32[1,2,256,384]{3,2,1,0:T(8,128)S(1)} copy-done((f32[1,2,256,384]{3,2,1,0:T(8,128)S(1)}, f32[1,2,256,384]{3,2,1,0:T(8,128)}, u32[]{:S(2)}) %copy-start) | copy-done | bytes 786456
  2.1 0.0 copy-start.1
  2.1 0.9 copy-done.1
  3.0 93.8 %shard_map.37 = f32[1,2,256,384]{3,2,1,0:T(8,128)S(1)} custom-call(bf16[1,256,384]{2,1,0:T(8,128)(2,1)S(1)} %copy-done.1, f32[1,2,256,384]{3,2,1,0:T(8,128)S(1)} %copy-done, s32[256]{0:T(256)S(1)} %reshape.3.disp_ref), custom_call_target="tpu_custom_call" | custom-call | tf_op jit(solution)/shard_map/pallas_call | solution.py:313
  96.8 0.9 copy.6
Async XLA Ops:
  1.0 1.1 %copy-start = (f32[1,2,256,384]{3,2,1,0:T(8,128)S(1)}, f32[1,2,256,384]{3,2,1,0:T(8,128)}, u32[]{:S(2)}) copy-start(f32[1,2,256,384]{3,2,1,0:T(8,128)} %field_ref.1) | copy-start | bytes 2359300
  2.1 0.9 copy-start.1

commit v2 on v1

--- a/solution.py
+++ b/solution.py
@@ -12,6 +12,15 @@
 CHUNK = 32
 PAD = 8
 OFFSETS = (1, 2, -1, -2)
+EXTRA = 4
+
+GROUP = (
+    (((1, 2), (2, 3), (-4, EXTRA)), (0, 1, EXTRA), (2, 3), {0: (2, 2), 1: (4, 3), EXTRA: (3, 0)}),
+    (((-1, 0), (2, 3)), (1, 2), (0, 3), {1: (4, 3)}),
+    (((1, 2), (-2, 1)), (0, 3), (2, 1), {3: (-4, 1)}),
+    (((-1, 0), (-2, 1), (4, EXTRA)), (2, 3, EXTRA), (0, 1), {2: (-2, 0), 3: (-4, 1), EXTRA: (-3, 2)}),
+)
+DIRECT = ((((-1, 0), (-2, 1), (1, 2), (2, 3)), (0, 1, 2, 3), (), {}),)
 
 charb_eps2 = 0.25
 step_size = 0.2
@@ -21,13 +30,15 @@
 
 
 def kernel(sections, tiles, image_ref, field_ref, disp_ref, out_ref, *scratch):
-    moved_refs = (scratch[0:4], scratch[4:8])
-    (warp_ref, u_ref, img_ref, grow_ref, gcol_ref, comb_ref, data_ref, own_ref, sum_ref, tile_slots, sec_slots) = scratch[8:19]
-    (img_send, img_recv, u_send, u_recv, w_send, w_recv, h_send, h_recv, t_send, t_recv, s_send, s_recv) = scratch[19:]
+    moved_refs = (scratch[0:5], scratch[5:10])
+    (warp_ref, u_ref, img_ref, grow_ref, gcol_ref, comb_ref, data_ref, own_ref, sum_ref, tile_slots, sec_slots) = scratch[10:21]
+    (img_send, img_recv, u_send, u_recv, w_send, w_recv, h_send, h_recv, r_send, t_send, t_recv, s_send, s_recv) = scratch[21:]
     rows, width = grow_ref.shape
     height = rows * tiles
     cols = width // BLOCK
     chunks = rows // CHUNK
+    pieces = rows // BLOCK
+    plan = GROUP if sections % len(GROUP) == 0 else DIRECT
     section = lax.axis_index("sec")
     tile = lax.axis_index("tile")
 
@@ -131,11 +142,18 @@
     def step(turn, p):
         refs = moved_refs[p]
 
-        def main_copy(i):
-            target = jnp.clip(section - OFFSETS[i], 0, sections - 1)
-            return remote(
-                warp_ref.at[p], refs[i].at[pl.ds(1, rows // BLOCK)], w_send.at[p, i], w_recv.at[p, i], target, tile
-            )
+        def source_of(place, i):
+            return OFFSETS[i] if i != EXTRA else (4 if place == 0 else -4)
+
+        def piece_copy(src, slot, q, send, offset):
+            target = jnp.minimum(jnp.maximum(section + offset, 0), sections - 1)
+            return remote(src, refs[slot].at[1 + q], send, w_recv.at[p, slot, q], target, tile)
+
+        def own_copy(offset, slot, q):
+            return piece_copy(warp_ref.at[p, q], slot, q, w_send.at[p, slot, q], offset)
+
+        def pass_copy(i, offset, slot, q):
+            return piece_copy(refs[i].at[1 + q], slot, q, r_send.at[p, i, q], offset)
 
         def relay_up(i):
             return remote(
@@ -149,15 +167,27 @@
                 h_send.at[p, i, 1], h_recv.at[p, i, 1], section, below,
             )
 
-        def start_main(i):
-            pl.when(in_stack(section - OFFSETS[i]))(main_copy(i).start)
-
-        def relay(i):
-            @pl.when(in_stack(section + OFFSETS[i]))
-            def _():
-                main_copy(i).wait_recv()
-                pl.when(has_above)(relay_up(i).start)
-                pl.when(has_below)(relay_down(i).start)
+        def start_own(place):
+            for q in range(pieces):
+                for offset, slot in plan[place][0]:
+                    pl.when(in_stack(section + offset))(own_copy(offset, slot, q).start)
+
+        def receive(place):
+            _, near, far, passes = plan[place]
+            for slots in (near, far):
+                for q in range(pieces):
+                    for i in slots:
+
+                        @pl.when(in_stack(section + source_of(place, i)))
+                        def _():
+                            own_copy(0, i, q).wait_recv()
+                            if i in passes:
+                                offset, slot = passes[i]
+                                pl.when(in_stack(section + offset))(pass_copy(i, offset, slot, q).start)
+                            if i != EXTRA and q == 0:
+                                pl.when(has_above)(relay_up(i).start)
+                            if i != EXTRA and q == pieces - 1:
+                                pl.when(has_below)(relay_down(i).start)
 
         def arrive(i):
             @pl.when(in_stack(section + OFFSETS[i]))
@@ -165,16 +195,26 @@
                 pl.when(has_below)(relay_up(i).wait_recv)
                 pl.when(has_above)(relay_down(i).wait_recv)
 
-        def finish(i):
-            pl.when(in_stack(section - OFFSETS[i]))(main_copy(i).wait_send)
-
+        def finish(place):
+            own, _, _, passes = plan[place]
+            for q in range(pieces):
+                for offset, slot in own:
+                    pl.when(in_stack(section + offset))(own_copy(offset, slot, q).wait_send)
+                for i, (offset, slot) in passes.items():
+                    has_both = in_stack(section + source_of(place, i)) & in_stack(section + offset)
+                    pl.when(has_both)(pass_copy(i, offset, slot, q).wait_send)
+
+        def finish_relay(i):
             @pl.when(in_stack(section + OFFSETS[i]))
             def _():
                 pl.when(has_above)(relay_up(i).wait_send)
                 pl.when(has_below)(relay_down(i).wait_send)
 
-        for i in range(4):
-            start_main(i)
+        def each_place(action):
+            for place in range(len(plan)):
+                pl.when(lax.rem(section, len(plan)) == place)(functools.partial(action, place))
+
+        each_place(start_own)
         edge_start(u_ref.at[p], u_send.at[p], u_recv.at[p])
 
         def count_one(s, total):
@@ -204,8 +244,7 @@
             resid = jnp.where(mask > 0, own - other, 0.0)
             return resid, resid * lax.rsqrt(resid * resid + charb_eps2)
 
-        relay(0)
-        relay(1)
+        each_place(receive)
         arrive(0)
         arrive(1)
         shifts = [shift_of(i) for i in range(4)]
@@ -231,8 +270,6 @@
 
         for d in range(1, tiles):
             tile_copy(d).start()
-        relay(2)
-        relay(3)
         total = own_ref[p]
         for d in range(1, tiles):
             tile_copy(d).wait_recv()
@@ -263,8 +300,9 @@
 
         chunk_loop(backward, 0)
 
+        each_place(finish)
         for i in range(4):
-            finish(i)
+            finish_relay(i)
         total = sum_ref[p]
         for d in range(1, sections):
             sec_copy(d).wait_recv()
@@ -319,7 +357,7 @@
                 pl.BlockSpec(memory_space=pltpu.SMEM),
             ],
             out_specs=pl.BlockSpec(memory_space=pltpu.VMEM),
-            scratch_shapes=[pltpu.VMEM((rows // BLOCK + 2, cols, BLOCK, BLOCK), jnp.bfloat16) for _ in range(8)]
+            scratch_shapes=[pltpu.VMEM((rows // BLOCK + 2, cols, BLOCK, BLOCK), jnp.bfloat16) for _ in range(10)]
             + [
                 pltpu.VMEM((2, rows // BLOCK, cols, BLOCK, BLOCK), jnp.bfloat16),
                 pltpu.VMEM((2, 2, rows + 2 * PAD, width), jnp.float32),
@@ -334,8 +372,9 @@
                 pltpu.VMEM((2, sections - 1, 8, BLOCK), jnp.float32),
                 dma((2,)), dma((2,)),
                 dma((2, 2)), dma((2, 2)),
-                dma((2, 4)), dma((2, 4)),
+                dma((2, 5, rows // BLOCK)), dma((2, 5, rows // BLOCK)),
                 dma((2, 4, 2)), dma((2, 4, 2)),
+                dma((2, 5, rows // BLOCK)),
                 dma((2, tiles - 1)), dma((2, tiles - 1)),
                 dma((2, sections - 1)), dma((2, sections - 1)),
             ],

time: 97.9 us -> 83.4 us (0.85)
  Pallas kernels: 93.8 us -> 79.3 us
    pallas_call x1, Pallas kernels: 93.8 us -> 79.3 us  [per_device(): pl.pallas_call(functools.partial(kernel, sections, tiles), out_shape=jax....]
where the time goes in v2:
time: 83.4 us; the launch traced here: 83.2 us
  Pallas kernels  79.3 us (95%)
  local copies, waits for them, and re-layouts  3.9 us (5%)
    pallas_call x1, Pallas kernels, per_device(): pl.pallas_call(functools.partial(kernel, sections, tiles), out_shape=jax....  79.3 us
    unnamed x6, local copies, waits for them, and re-layouts  3.76 us

profile of v2, /device:TPU:0, one launch (start us, length us, event | category | flops | bytes accessed | tf_op | source)
XLA Modules:
  0.0 83.2 jit_solution(11940496657827964690)
XLA Ops:
  0.0 0.8 copy.4
  0.8 0.1 reshape.3.disp_ref
  1.0 0.0 copy-start
  1.0 1.1 %copy-done = f32[1,2,256,384]{3,2,1,0:T(8,128)S(1)} copy-done((f32[1,2,256,384]{3,2,1,0:T(8,128)S(1)}, f32[1,2,256,384]{3,2,1,0:T(8,128)}, u32[]{:S(2)}) %copy-start) | copy-done | bytes 786456
  2.1 0.0 copy-start.1
  2.1 0.9 %copy-done.1 = bf16[1,256,384]{2,1,0:T(8,128)(2,1)S(1)} copy-done((bf16[1,256,384]{2,1,0:T(8,128)(2,1)S(1)}, bf16[1,256,384]{2,1,0:T(8,128)(2,1)}, u32[]{:S(2)}) %copy-start.1) | copy-done | bytes 196632
  3.0 79.3 %shard_map.37 = f32[1,2,256,384]{3,2,1,0:T(8,128)S(1)} custom-call(bf16[1,256,384]{2,1,0:T(8,128)(2,1)S(1)} %copy-done.1, f32[1,2,256,384]{3,2,1,0:T(8,128)S(1)} %copy-done, s32[256]{0:T(256)S(1)} %reshape.3.disp_ref), custom_call_target="tpu_custom_call" | custom-call | tf_op jit(solution)/shard_map/pallas_call | solution.py:351
  82.3 0.9 %copy.6 = f32[1,2,256,384]{3,2,1,0:T(8,128)} copy(f32[1,2,256,384]{3,2,1,0:T(8,128)S(1)} %shard_map.37) | data formatting | bytes 1572864
Async XLA Ops:
  1.0 1.1 %copy-start = (f32[1,2,256,384]{3,2,1,0:T(8,128)S(1)}, f32[1,2,256,384]{3,2,1,0:T(8,128)}, u32[]{:S(2)}) copy-start(f32[1,2,256,384]{3,2,1,0:T(8,128)} %field_ref.1) | copy-start | bytes 2359300
  2.1 0.9 %copy-start.1 = (bf16[1,256,384]{2,1,0:T(8,128)(2,1)S(1)}, bf16[1,256,384]{2,1,0:T(8,128)(2,1)}, u32[]{:S(2)}) copy-start(bf16[1,256,384]{2,1,0:T(8,128)(2,1)} %image_ref.1) | copy-start | bytes 589828

commit v3 on v2

--- a/solution.py
+++ b/solution.py
@@ -9,7 +9,7 @@
 
 BLOCK = 128
 ITERS = 4
-CHUNK = 32
+CHUNK = 64
 PAD = 8
 OFFSETS = (1, 2, -1, -2)
 EXTRA = 4
@@ -102,7 +102,6 @@
 
     pl.semaphore_wait(barrier, sections - 1 + tiles - 1)
     edge_start(img_ref, img_send, img_recv)
-    edge_wait(img_ref, img_send, img_recv)
 
     def block_of(c):
         block = c // (BLOCK // CHUNK)
@@ -134,7 +133,13 @@
         store_warp(0, c, base, grow, gcol, u0, u1)
         return carry
 
-    chunk_loop(first_warp, 0)
+    def inner_warp(c, carry):
+        return first_warp(c, pl.multiple_of(c * CHUNK, CHUNK), carry)
+
+    lax.fori_loop(1, chunks - 1, inner_warp, 0)
+    edge_wait(img_ref, img_send, img_recv)
+    first_warp(0, 0, 0)
+    first_warp(chunks - 1, rows - CHUNK, 0)
 
     def in_stack(at):
         return (at >= 0) & (at < sections)

time: 83.4 us -> 82.2 us (0.986)
  Pallas kernels: 79.3 us -> 78.1 us
    pallas_call x1, Pallas kernels: 79.3 us -> 78.1 us  [per_device(): pl.pallas_call(functools.partial(kernel, sections, tiles), out_shape=jax....]
where the time goes in v3:
time: 82.2 us; the launch traced here: 82 us
  Pallas kernels  78.1 us (95%)
  local copies, waits for them, and re-layouts  3.9 us (5%)
    pallas_call x1, Pallas kernels, per_device(): pl.pallas_call(functools.partial(kernel, sections, tiles), out_shape=jax....  78.1 us
    unnamed x6, local copies, waits for them, and re-layouts  3.76 us

profile of v3, /device:TPU:0, one launch (start us, length us, event | category | flops | bytes accessed | tf_op | source)
XLA Modules:
  0.0 82.0 jit_solution(6257021519818184856)
XLA Ops:
  0.0 0.8 copy.4
  0.8 0.1 reshape.3.disp_ref
  1.0 0.0 copy-start
  1.0 1.1 %copy-done = f32[1,2,256,384]{3,2,1,0:T(8,128)S(1)} copy-done((f32[1,2,256,384]{3,2,1,0:T(8,128)S(1)}, f32[1,2,256,384]{3,2,1,0:T(8,128)}, u32[]{:S(2)}) %copy-start) | copy-done | bytes 786456
  2.1 0.0 copy-start.1
  2.1 0.9 %copy-done.1 = bf16[1,256,384]{2,1,0:T(8,128)(2,1)S(1)} copy-done((bf16[1,256,384]{2,1,0:T(8,128)(2,1)S(1)}, bf16[1,256,384]{2,1,0:T(8,128)(2,1)}, u32[]{:S(2)}) %copy-start.1) | copy-done | bytes 196632
  3.0 78.1 %shard_map.37 = f32[1,2,256,384]{3,2,1,0:T(8,128)S(1)} custom-call(bf16[1,256,384]{2,1,0:T(8,128)(2,1)S(1)} %copy-done.1, f32[1,2,256,384]{3,2,1,0:T(8,128)S(1)} %copy-done, s32[256]{0:T(256)S(1)} %reshape.3.disp_ref), custom_call_target="tpu_custom_call" | custom-call | tf_op jit(solution)/shard_map/pallas_call | solution.py:356
  81.1 0.9 %copy.6 = f32[1,2,256,384]{3,2,1,0:T(8,128)} copy(f32[1,2,256,384]{3,2,1,0:T(8,128)S(1)} %shard_map.37) | data formatting | bytes 1572864
Async XLA Ops:
  1.0 1.1 %copy-start = (f32[1,2,256,384]{3,2,1,0:T(8,128)S(1)}, f32[1,2,256,384]{3,2,1,0:T(8,128)}, u32[]{:S(2)}) copy-start(f32[1,2,256,384]{3,2,1,0:T(8,128)} %field_ref.1) | copy-start | bytes 2359300
  2.1 0.9 %copy-start.1 = (bf16[1,256,384]{2,1,0:T(8,128)(2,1)S(1)}, bf16[1,256,384]{2,1,0:T(8,128)(2,1)}, u32[]{:S(2)}) copy-start(bf16[1,256,384]{2,1,0:T(8,128)(2,1)} %image_ref.1) | copy-start | bytes 589828
